TPU v7x, 256 devices: a whole 4x4x8 slice. The times are simulated.
256 devices in a mesh: pb: 8 (over x, core), pq: 32 (over z, y).
Axes of the slice: x: 4, y: 4, z: 8, core: 2. Of those that a mesh axis runs over, the one named last changes fastest.
Arguments:
- chol_vv: bfloat16 [352, 1792, 1792], P('pb', 'pq'), may hold values from -6 to 6
- chol_ov: bfloat16 [352, 256, 1792], P('pb', 'pq'), may hold values from -6 to 6
- chol_oo: bfloat16 [352, 256, 256], P('pb', 'pq'), may hold values from -6 to 6
- chol_vo: bfloat16 [352, 256, 1792], P('pb', None, 'pq'), may hold values from -6 to 6
- amplitudes: bfloat16 [256, 1792], P(None, 'pq'), may hold values from -0.125 to 0.125
Outputs:
- dressed: bfloat16 [352, 256, 1792], P('pb', 'pq')
- fock_ov: float32 [256, 1792], P('pq')
All inputs are finite; a program needn't handle non-finite values.
Results may differ from a plain program's by a relative error of at most 0.0081.
Values may be sent and summed in bfloat16 or wider, within the bound.
A program may use at most 64 MiB of HBM per device.

v0:
```python
import jax
import jax.numpy as jnp
from jax import lax
from jax.sharding import PartitionSpec as P


def laid_out(blocks, dim):
    dims = list(blocks.shape[1:])
    dims[dim] *= blocks.shape[0]
    return jnp.moveaxis(blocks, 0, dim).reshape(dims)


def copy_for_each(shard, axis):
    copies = jnp.broadcast_to(shard, (lax.axis_size(axis), *shard.shape))
    return lax.all_to_all(copies, axis, split_axis=0, concat_axis=0, tiled=True)


def gathered_copies(shard, axis, dim):
    return laid_out(copy_for_each(shard, axis), dim)


def taken_together(shard, axis):
    everything = copy_for_each(shard, axis)
    return jnp.sum(everything, axis=0)


def per_device(chol_vv, chol_ov, chol_oo, chol_vo, amplitudes):
    batch = chol_vv.shape[0]
    occ_rows = chol_ov.shape[1]
    whole_amps = gathered_copies(amplitudes, "pq", 1)
    lprime = (
        chol_oo.astype(jnp.float32)
        + jnp.einsum("qjb,ib->qji", chol_ov, whole_amps, preferred_element_type=jnp.float32)
    ).astype(jnp.bfloat16)
    direct = jnp.einsum("qab,ib->qia", chol_vv, whole_amps, preferred_element_type=jnp.float32)
    partial_sum = chol_vo.astype(jnp.float32) + direct
    moved_sum = lax.all_to_all(
        partial_sum.astype(jnp.bfloat16), "pq", split_axis=1, concat_axis=2, tiled=True
    ).astype(partial_sum.dtype)
    moved_lprime = lax.all_to_all(lprime, "pq", split_axis=2, concat_axis=1, tiled=True)
    occupied = jnp.einsum(
        "qji,ja->qia", moved_lprime, whole_amps, preferred_element_type=jnp.float32
    )
    dressed = (moved_sum - occupied).astype(jnp.bfloat16)
    row_start = lax.axis_index("pq") * occ_rows
    own_amps = lax.dynamic_slice_in_dim(whole_amps, row_start, occ_rows, 0)
    local_coulomb = 2.0 * jnp.einsum(
        "qia,ia->q", dressed, own_amps, preferred_element_type=jnp.float32
    )
    coulomb = taken_together(local_coulomb, "pq")
    local_fock = jnp.sum(coulomb[:, None, None] * dressed.astype(jnp.float32), axis=0)
    fock_ov = taken_together(local_fock, "pb") / (batch * lax.axis_size("pb"))
    return (dressed, fock_ov)


def solution(mesh):
    in_specs = (
        P("pb", "pq", None),
        P("pb", "pq", None),
        P("pb", "pq", None),
        P("pb", None, "pq"),
        P(None, "pq"),
    )
    out_specs = (P("pb", "pq", None), P("pq", None))
    return jax.shard_map(
        per_device, mesh=mesh, in_specs=in_specs, out_specs=out_specs, check_vma=False
    )
```

profile of v0, /device:TPU:1, one launch (start us, length us, event | category | flops | bytes accessed | tf_op | source)
XLA Modules:
  0.0 155.8 jit_solution(2458996371990854179)
XLA Ops:
  0.6 0.0 copy-start
  0.6 0.0 copy-start.2
  0.7 0.9 broadcast_in_dim.10
  1.6 35.4 %all_to_all.43 = bf16[32,256,56]{1,2,0:T(8,128)(2,1)S(1)} all-to-all(bf16[32,256,56]{1,2,0:T(8,128)(2,1)S(1)} %broadcast_in_dim.10), channel_id=1, replica_groups=mesh['pb'=8,'pq'=32] {'pq'}, dimensions={0} | all-to-all | bytes 1835008 | tf_op jit(solution)/shard_map/all_to_all | solution.py:15
  37.0 0.0 copy-done
  37.0 0.0 copy-done.2
  37.0 0.5 fusion.4
  37.5 0.4 copy.53
  37.9 1.9 %reshape.26 = bf16[32,2,1408]{2,1,0:T(2,128)(2,1)} reshape(bf16[256,8,44]{2,1,0:T(8,128)(2,1)S(1)} %bitcast.46) | data formatting | bytes 360448
  39.8 6.1 %all-to-all-start.2 = ((bf16[32,2,1408]{2,1,0:T(2,128)(2,1)}), bf16[32,2,1408]{2,1,0:T(2,128)(2,1)}, u32[]{:S(2)}, u32[]{:S(2)}) async-start(bf16[32,2,1408]{2,1,0:T(2,128)(2,1)} %reshape.26), calls=%async_computation.2 | async-start | bytes 360448 | tf_op jit(solution)/shard_map/all_to_all | solution.py:40
  45.9 6.3 %fusion.1 = bf16[44,256,56]{1,2,0:T(8,128)(2,1)S(1)} fusion(bf16[44,256,56]{1,2,0:T(8,128)(2,1)} %param.8, bf16[256,1792,1]{0,1,2:T(8,128)(2,1)S(1)} %bitcast.43, bf16[44,56,1792]{2,1,0:T(8,128)(2,1)} %param.5), kind=kOutput, calls=%fused_computation.4 | convolution fusion | flops 2262622208 | bytes 12271616 | tf_op jit(solution)/shard_map/qab,ib->qia/dot_general | solution.py:35
  52.2 4.5 %copy.49 = bf16[44,256,56]{2,0,1:T(8,128)(2,1)} copy(bf16[44,256,56]{1,2,0:T(8,128)(2,1)S(1)} %fusion.1) | data formatting | bytes 2523136 | tf_op jit(solution)/shard_map/convert_element_type | solution.py:38
  56.7 6.4 %reshape.24 = bf16[32,2,9856]{2,1,0:T(2,128)(2,1)} reshape(bf16[256,44,56]{2,1,0:T(8,128)(2,1)} %bitcast.41) | data formatting | bytes 2523136
  63.1 0.0 all-to-all-done.2
  63.1 9.3 %all-to-all-start.1 = ((bf16[32,2,9856]{2,1,0:T(2,128)(2,1)}), bf16[32,2,9856]{2,1,0:T(2,128)(2,1)S(1)}, u32[]{:S(2)}, u32[]{:S(2)}) async-start(bf16[32,2,9856]{2,1,0:T(2,128)(2,1)} %reshape.24), calls=%async_computation.1 | async-start | bytes 2523136 | tf_op jit(solution)/shard_map/all_to_all | solution.py:37
  72.4 1.0 dynamic-slice_bitcast_fusion
  73.4 1.3 copy.63
  74.7 3.2 %reshape.27 = bf16[256,8,44]{2,1,0:T(8,128)(2,1)} reshape(bf16[32,2,1408]{2,1,0:T(2,128)(2,1)} %all-to-all-done.2) | data formatting | bytes 360448
  77.9 2.0 %copy.55 = bf16[44,32,8,8]{0,3,2,1:T(8,128)(2,1)} copy(bf16[44,32,8,8]{0,2,3,1:T(8,128)(2,1)} %bitcast.47) | data formatting | bytes 360448 | tf_op jit(solution)/shard_map/all_to_all | solution.py:40
  79.8 2.2 %copy.56 = bf16[44,256,8]{1,2,0:T(8,128)(2,1)} copy(bf16[44,256,8]{0,2,1:T(8,128)(2,1)} %bitcast.48) | data formatting | bytes 360448 | tf_op jit(solution)/shard_map/all_to_all | solution.py:40
  82.0 19.5 %all-to-all-done.1 = bf16[32,2,9856]{2,1,0:T(2,128)(2,1)S(1)} async-done(((bf16[32,2,9856]{2,1,0:T(2,128)(2,1)}), bf16[32,2,9856]{2,1,0:T(2,128)(2,1)S(1)}, u32[]{:S(2)}, u32[]{:S(2)}) %all-to-all-start.1) | async-done | bytes 1261600 | tf_op jit(solution)/shard_map/all_to_all | solution.py:37
  101.5 5.6 %reshape.25 = bf16[256,44,56]{2,1,0:T(8,128)(2,1)} reshape(bf16[32,2,9856]{2,1,0:T(2,128)(2,1)S(1)} %all-to-all-done.1) | data formatting | bytes 2523136
  107.1 2.6 %convert_bitcast_fusion = f32[44,8,32,56]{3,1,2,0:T(8,128)S(1)} fusion(bf16[44,256,56]{2,0,1:T(8,128)(2,1)} %bitcast.40), kind=kLoop, calls=%fused_computation | loop fusion | flops 630784 | bytes 3784704 | tf_op jit(solution)/shard_map/convert_element_type | solution.py:39
  109.7 3.6 %copy.51 = f32[44,8,32,56]{3,2,1,0:T(8,128)} copy(f32[44,8,32,56]{3,1,2,0:T(8,128)S(1)} %convert_bitcast_fusion) | data formatting | bytes 5046272 | tf_op jit(solution)/shard_map/convert_element_type | solution.py:39
  113.4 6.3 %reshape.17 = f32[44,8,1792]{2,1,0:T(8,128)} reshape(f32[44,8,32,56]{3,2,1,0:T(8,128)} %copy.51) | data formatting | bytes 5046272 | tf_op jit(solution)/shard_map/convert_element_type | solution.py:39
  119.7 2.3 %fusion = bf16[44,8,1792]{2,1,0:T(8,128)(2,1)S(1)} fusion(f32[44,8,1792]{2,1,0:T(8,128)} %reshape.17, bf16[44,256,8]{1,2,0:T(8,128)(2,1)} %copy.56, bf16[256,1792,1]{0,1,2:T(8,128)(2,1)S(1)} %bitcast.45), kind=kOutput, calls=%fused_computation.2 | convolution fusion | flops 324222976 | bytes 4882432 | tf_op jit(solution)/shard_map/qji,ja->qia/dot_general | solution.py:41
  122.0 0.0 copy-start.1
  122.0 0.5 fusion.8
  122.5 15.3 %all_to_all.44 = f32[32,1,44]{2,1,0:T(1,128)S(1)} all-to-all(f32[32,1,44]{2,1,0:T(1,128)S(1)} %broadcast_in_dim.11), channel_id=1, replica_groups=mesh['pb'=8,'pq'=32] {'pq'}, dimensions={0} | all-to-all | bytes 11264 | tf_op jit(solution)/shard_map/all_to_all | solution.py:15
  137.8 0.3 multiply_reduce_fusion
  138.2 16.9 %all_to_all.45 = f32[8,8,1792]{2,1,0:T(8,128)S(1)} all-to-all(f32[8,8,1792]{2,1,0:T(8,128)S(1)} %broadcast_in_dim.12), channel_id=1, replica_groups=mesh['pb'=8,'pq'=32] {'pb'}, dimensions={0} | all-to-all | bytes 917504 | tf_op jit(solution)/shard_map/all_to_all | solution.py:15
  155.1 0.0 copy-done.1
  155.1 0.6 broadcast_multiply_fusion
  (4 shorter events, 0.1 us)
Async XLA Ops:
  0.6 36.4 %copy-start = (bf16[44,8,1792]{2,1,0:T(8,128)(2,1)S(1)}, bf16[44,8,1792]{2,1,0:T(8,128)(2,1)}, u32[]{:S(2)}) copy-start(bf16[44,8,1792]{2,1,0:T(8,128)(2,1)} %param.6) | copy-start | bytes 3784708
  0.6 36.4 %copy-start.2 = (bf16[44,8,256]{2,1,0:T(8,128)(2,1)S(1)}, bf16[44,8,256]{2,1,0:T(8,128)(2,1)}, u32[]{:S(2)}) copy-start(bf16[44,8,256]{2,1,0:T(8,128)(2,1)} %param.7) | copy-start | bytes 540676
  39.8 23.3 %all-to-all-start.2 = ((bf16[32,2,1408]{2,1,0:T(2,128)(2,1)}), bf16[32,2,1408]{2,1,0:T(2,128)(2,1)}, u32[]{:S(2)}, u32[]{:S(2)}) async-start(bf16[32,2,1408]{2,1,0:T(2,128)(2,1)} %reshape.26), calls=%async_computation.2 | async-start | bytes 360448 | tf_op jit(solution)/shard_map/all_to_all | solution.py:40
  63.1 38.4 %all-to-all-start.1 = ((bf16[32,2,9856]{2,1,0:T(2,128)(2,1)}), bf16[32,2,9856]{2,1,0:T(2,128)(2,1)S(1)}, u32[]{:S(2)}, u32[]{:S(2)}) async-start(bf16[32,2,9856]{2,1,0:T(2,128)(2,1)} %reshape.24), calls=%async_computation.1 | async-start | bytes 2523136 | tf_op jit(solution)/shard_map/all_to_all | solution.py:37
  122.0 33.1 %copy-start.1 = (bf16[44,8,1792]{2,1,0:T(8,128)(2,1)}, bf16[44,8,1792]{2,1,0:T(8,128)(2,1)S(1)}, u32[]{:S(2)}) copy-start(bf16[44,8,1792]{2,1,0:T(8,128)(2,1)S(1)} %fusion) | copy-start | bytes 3784708
where the time goes:
time: 157 us; the launch traced here: 156 us
  blocking collectives  67.6 us (43%)
  local copies, waits for them, and re-layouts  39.2 us (25%)
  waiting for transfers between devices  19.5 us (12%)
  starting transfers between devices  15.4 us (10%)
  matrix products  9.58 us (6%)
  other arithmetic  3.61 us (2%)
    all_to_all x3, blocking collectives, copy_for_each(): return lax.all_to_all(copies, axis, split_axis=0, concat_axis=0, tiled=True)  67.6 us
    all_to_all x1, waiting for transfers between devices, per_device(): lax.all_to_all(partial_sum.astype(jnp.bfloat16), 'pq', split_axis=1, conc...  19.5 us
    unnamed x10, local copies, waits for them, and re-layouts  17.1 us
    convert_element_type x2, local copies, waits for them, and re-layouts, per_device(): moved_sum = lax.all_to_all(partial_sum.astype(jnp.bfloat16), 'pq', split_...  9.91 us
    all_to_all x1, starting transfers between devices, per_device(): lax.all_to_all(partial_sum.astype(jnp.bfloat16), 'pq', split_axis=1, conc...  9.33 us
    dot_general x1, matrix products, per_device(): jnp.einsum('qab,ib->qia', chol_vv, whole_amps, preferred_element_type=jnp...  6.27 us
    all_to_all x1, starting transfers between devices, per_device(): lax.all_to_all(lprime, 'pq', split_axis=2, concat_axis=1, tiled=True)  6.1 us
    convert_element_type x1, local copies, waits for them, and re-layouts, per_device(): partial_sum.astype(jnp.bfloat16)  4.5 us
  transfers between devices with their start and end apart: 2, of which 1 were waited for; matrix products, arithmetic and copies ran while one was open for 17% of the time, Pallas kernels for 0%

commit v1 on v0

v1 whole, which is shorter than its diff:
```python
import jax
import jax.numpy as jnp
from jax import lax
from jax.experimental import pallas as pl
from jax.experimental.pallas import tpu as pltpu
from jax.sharding import PartitionSpec as P

BF, F32 = jnp.bfloat16, jnp.float32
MESH = pl.DeviceIdType.MESH
NZ, NY, NPB = 8, 4, 8
NPQ = NZ * NY
NOCC, NVIRT, QB = 256, 1792, 44
AB, JB = NVIRT // NPQ, NOCC // NPQ
LP_OFF = 672
ROWS = 224
ZORDER = (1, 7, 2, 6, 3, 5, 4)


def dot_t(a, b):
    return lax.dot_general(a, b, (((1,), (1,)), ((), ())), preferred_element_type=F32)


def kernel(vv, ov, oo, vo, am, dressed, fock_out,
           vv_v, ov_v, oo_v, vo_v, t_own, slots, tmat, dbuf, send_a, send_b, recv_a, recv_b,
           lp, occ, dr, fock, fock_r, coul_s, coul_r, coul_b, pq,
           lsem, zsend, zrecv, ysend, yrecv, csend, crecv, msend, mrecv, qsend, qrecv, fsend, frecv, osem):
    pb, me = lax.axis_index("pb"), lax.axis_index("pq")
    z, y = me // NY, me % NY
    half = pb % 2
    partner = pb + 1 - 2 * half

    def zpeer(d):
        return lax.rem(z + d, NZ) * NY + y

    def ypeer(d):
        return z * NY + lax.rem(y + d, NY)

    bar = pltpu.get_barrier_semaphore()
    for d in range(1, NZ):
        pl.semaphore_signal(bar, inc=1, device_id=(pb, zpeer(d)), device_id_type=MESH)
    for d in range(1, NY):
        pl.semaphore_signal(bar, inc=1, device_id=(pb, ypeer(d)), device_id_type=MESH)
    for d in range(1, NPB):
        pl.semaphore_signal(bar, inc=1, device_id=(lax.rem(pb + d, NPB), me), device_id_type=MESH)

    own_slot = y * NZ + z
    loads = [
        pltpu.make_async_copy(
            am.at[:, :, pl.ds(pl.multiple_of(128 * half, 128), 128)], slots.at[half, own_slot], lsem.at[0]),
        pltpu.make_async_copy(am, t_own, lsem.at[1]),
        pltpu.make_async_copy(oo, oo_v, lsem.at[2]),
        pltpu.make_async_copy(ov, ov_v, lsem.at[3]),
        pltpu.make_async_copy(vo, vo_v, lsem.at[4]),
        pltpu.make_async_copy(vv, vv_v, lsem.at[5]),
    ]
    for c in loads:
        c.start()
    loads[0].wait()
    pl.semaphore_wait(bar, (NZ - 1) + (NY - 1) + (NPB - 1))

    def z_copy(d):
        return pltpu.make_async_remote_copy(
            src_ref=slots.at[half, own_slot], dst_ref=slots.at[half, own_slot],
            send_sem=zsend, recv_sem=zrecv.at[d - 1], device_id=(pb, zpeer(d)), device_id_type=MESH)

    for d in ZORDER:
        z_copy(d).start()

    def y_copy(slot, d):
        return pltpu.make_async_remote_copy(
            src_ref=slots.at[half, slot], dst_ref=slots.at[half, slot],
            send_sem=ysend, recv_sem=yrecv.at[d - 1], device_id=(pb, ypeer(d)), device_id_type=MESH)

    for d in range(1, NY):
        y_copy(own_slot, d).start()
    for d in ZORDER:
        z_copy(d).wait_recv()
        slot = y * NZ + lax.rem(z + NZ - d, NZ)
        for e in range(1, NY):
            y_copy(slot, e).start()

    def c_copy(e):
        group = pl.ds(lax.rem(y + NY - e, NY) * NZ, NZ)
        return pltpu.make_async_remote_copy(
            src_ref=slots.at[half, group], dst_ref=slots.at[half, group],
            send_sem=csend, recv_sem=crecv.at[e], device_id=(partner, me), device_id_type=MESH)

    c_copy(0).start()

    for e in range(1, NY):
        group = pl.ds(lax.rem(y + NY - e, NY) * NZ, NZ)
        pltpu.make_async_copy(slots.at[half, group], slots.at[half, group], yrecv.at[e - 1]).wait()
        c_copy(e).start()
    for e in range(NY):
        group = pl.ds(lax.rem(y + NY - e, NY) * NZ, NZ)
        pltpu.make_async_copy(slots.at[1 - half, group], slots.at[1 - half, group], crecv.at[e]).wait()

    def widen(u, carry):
        for hh in range(2):
            for k in range(7):
                parts = []
                for g in (2 * k, 2 * k + 1):
                    p = 2 * u + g // 7
                    slot = lax.rem(p, NY) * NZ + p // NY
                    parts.append(slots[hh, slot, g % 7].astype(F32))
                tmat[pl.ds(pl.multiple_of(112 * u + 16 * k, 16), 16), 128 * hh:128 * hh + 128] = (
                    jnp.concatenate(parts, axis=0).astype(BF))
        return carry

    lax.fori_loop(0, NPQ // 2, widen, 0)

    def all_peer(k):
        return lax.rem(z + k // NY, NZ) * NY + lax.rem(y + k % NY, NY)

    def send_chunk(src, dst, c):
        def body(k, carry):
            peer = all_peer(k)
            pltpu.make_async_remote_copy(
                src_ref=src.at[peer], dst_ref=dst.at[me], send_sem=msend.at[c], recv_sem=mrecv.at[c],
                device_id=(pb, peer), device_id_type=MESH).start()
            return carry
        lax.fori_loop(1, NPQ, body, 0)
        dst[me] = src[me]

    for c in loads[1:]:
        c.wait()
    tw = t_own[...].astype(F32).reshape(1, AB // 8, 8, NOCC)

    def direct(row0, steps, q0):
        def body(s, carry):
            base = pl.multiple_of(s * ROWS, ROWS)
            rows = pl.ds(pl.multiple_of(row0 + base, 32), ROWS)
            d = vo_v[rows, :].astype(F32) + jnp.dot(vv_v[rows, :], tmat[...], preferred_element_type=F32)
            dbuf[pl.ds(base, ROWS), :] = d
            w = jnp.sum(d.reshape(ROWS // AB, AB // 8, 8, NOCC) * tw, axis=1)
            pq[pl.ds(q0 + s * (ROWS // AB), ROWS // AB)] = w[:, :, :128] + w[:, :, 128:]
            return carry
        lax.fori_loop(0, steps, body, 0)

    def ship(tiles, store):
        def body(t, carry):
            at = pl.multiple_of(t * 128, 128)
            store(at, dbuf[pl.ds(at, 128), :].T.reshape(NPQ, 8, 128).astype(BF))
            return carry
        lax.fori_loop(0, tiles, body, 0)

    lpr = oo_v[...].astype(F32) + jnp.dot(ov_v[...], tmat[...], preferred_element_type=F32)
    dbuf[LP_OFF:LP_OFF + 352, :] = lpr
    direct(0, 3, 0)

    def store_a(at, v):
        send_a[:, :, pl.ds(at, 128)] = v

    ship(8, store_a)
    send_chunk(send_a, recv_a, 0)
    lpr = dbuf[LP_OFF:LP_OFF + 352, :].astype(BF).astype(F32)

    def rest(c, carry):
        direct(672 + 896 * c, 4, 12 + 16 * c)

        def store_b(at, v):
            send_b[c, :, :, pl.ds(at, 128)] = v

        ship(7, store_b)
        send_chunk(send_b.at[c], recv_b.at[c], 1 + c)
        return carry

    pick = (lax.broadcasted_iota(jnp.int32, (8, NOCC), 1)
            == me * 8 + lax.broadcasted_iota(jnp.int32, (8, NOCC), 0)).astype(BF)
    own_rows = dot_t(pick, tmat[...]).astype(BF)
    gram = jnp.dot(own_rows, tmat[...], preferred_element_type=F32)
    w = lpr.reshape(QB, 8, NOCC) * gram[None]
    w = w[:, :, :128] + w[:, :, 128:]
    lax.fori_loop(0, 2, rest, 0)

    tot = jnp.sum(pq[...] - w, axis=1)
    tot = jnp.sum(tot, axis=1, keepdims=True)
    eye_q = (lax.broadcasted_iota(jnp.int32, (QB, 128), 0)
             == lax.broadcasted_iota(jnp.int32, (QB, 128), 1)).astype(F32)
    coul_s[0] = jnp.sum(eye_q * tot, axis=0, keepdims=True)

    def q_send(k, carry):
        peer = all_peer(k)
        pltpu.make_async_remote_copy(
            src_ref=coul_s.at[0], dst_ref=coul_r.at[me], send_sem=qsend, recv_sem=qrecv,
            device_id=(pb, peer), device_id_type=MESH).start()
        return carry

    lax.fori_loop(1, NPQ, q_send, 0)
    coul_r[me] = coul_s[0]

    lane = lax.broadcasted_iota(jnp.int32, (8, 128), 1)

    def wait_chunk(dst, c):
        part = dst.at[pl.ds(0, NPQ - 1)]
        pltpu.make_async_copy(part, part, mrecv.at[c]).wait()

    wait_chunk(recv_a, 0)

    def lp_row(q, carry):
        start = LP_OFF + 8 * q
        at = pl.multiple_of(start // 128 * 128, 128)
        off = start % 128
        for hh in range(2):
            acc = None
            for g in range(16):
                v = recv_a[16 * hh + g, :, pl.ds(at, 128)].astype(F32)
                v = pltpu.roll(v, lax.rem(8 * g - off + 128, 128), 1)
                acc = v if acc is None else jnp.where(lane >= 8 * g, v, acc)
            lp[pl.ds(pl.multiple_of(q * 8, 8), 8), 128 * hh:128 * hh + 128] = acc
        return carry

    lax.fori_loop(0, QB, lp_row, 0)
    for n in range(7):
        occ[:, 256 * n:256 * n + 256] = dot_t(lp[...].astype(BF), tmat[256 * n:256 * n + 256, :])

    pltpu.make_async_copy(coul_r.at[pl.ds(0, NPQ - 1)], coul_r.at[pl.ds(0, NPQ - 1)], qrecv).wait()
    coul = 2.0 * jnp.sum(coul_r[...].reshape(NPQ, 128), axis=0, keepdims=True)
    coul_b[...] = jnp.broadcast_to(jnp.sum(eye_q * coul, axis=1, keepdims=True), (QB, 128))

    fock[...] = jnp.zeros((8, NVIRT), F32)

    def gather_q(load, ql, q):
        start = AB * ql
        at = pl.multiple_of(start // 128 * 128, 128)
        nxt = pl.multiple_of(lax.min(at + 128, 768), 128)
        off = start % 128
        tiles = [None] * 14
        for p in range(NPQ):
            dst = AB * p
            o, t = dst % 128, dst // 128
            lo, hi = load(p, at), load(p, nxt)
            sh = lax.rem(o - off + 128, 128)
            lo, hi = pltpu.roll(lo, sh, 1), pltpu.roll(hi, sh, 1)
            src_lane = lax.rem(lane + (128 - o), 128) + off
            v = jnp.where(src_lane < 128, lo, hi)
            if tiles[t] is None:
                tiles[t] = v
            else:
                tiles[t] = jnp.where(lane >= o, v, tiles[t])
            if o + AB > 128:
                tiles[t + 1] = v
        cq = coul_b[pl.ds(q, 1), :]
        rows = pl.ds(pl.multiple_of(q * 8, 8), 8)
        for t in range(14):
            sl = slice(128 * t, 128 * t + 128)
            d = (tiles[t] - occ[rows, sl]).astype(BF)
            dr[q, :, sl] = d
            fock[:, sl] += cq * d.astype(F32)

    def do_a(ql, carry):
        gather_q(lambda p, at: recv_a[p, :, pl.ds(at, 128)].astype(F32), ql, ql)
        return carry

    lax.fori_loop(0, 12, do_a, 0)

    def do_b(c, carry):
        wait_chunk(recv_b.at[c], 1 + c)

        def inner(ql, carry2):
            gather_q(lambda p, at: recv_b[c, p, :, pl.ds(at, 128)].astype(F32), ql, 12 + 16 * c + ql)
            return carry2

        lax.fori_loop(0, 16, inner, 0)
        return carry

    lax.fori_loop(0, 2, do_b, 0)

    out = pltpu.make_async_copy(dr, dressed, osem)
    out.start()

    def f_copy(d):
        return pltpu.make_async_remote_copy(
            src_ref=fock, dst_ref=fock_r.at[pb], send_sem=fsend, recv_sem=frecv,
            device_id=(lax.rem(pb + d, NPB), me), device_id_type=MESH)

    for d in range(1, NPB):
        f_copy(d).start()
    fock_r[pb] = fock[...]
    part = fock_r.at[pl.ds(0, NPB - 1)]
    pltpu.make_async_copy(part, part, frecv).wait()
    fock_out[...] = jnp.sum(fock_r[...], axis=0) * (1.0 / (QB * NPB))

    out.wait()
    zs = slots.at[0, pl.ds(0, NZ - 1)]
    pltpu.make_async_copy(zs, zs, zsend).wait()
    ys = slots.at[0, pl.ds(0, NZ * (NY - 1))]
    pltpu.make_async_copy(ys, ys, ysend).wait()
    cs = slots.at[0]
    pltpu.make_async_copy(cs, cs, csend).wait()
    for c, src in ((0, recv_a), (1, recv_b.at[0]), (2, recv_b.at[1])):
        sp = src.at[pl.ds(0, NPQ - 1)]
        pltpu.make_async_copy(sp, sp, msend.at[c]).wait()
    qp = coul_r.at[pl.ds(0, NPQ - 1)]
    pltpu.make_async_copy(qp, qp, qsend).wait()
    pltpu.make_async_copy(part, part, fsend).wait()


def per_device(chol_vv, chol_ov, chol_oo, chol_vo, amplitudes):
    vv = chol_vv.reshape(QB * AB, NVIRT)
    ov = chol_ov.reshape(QB * JB, NVIRT)
    oo = chol_oo.reshape(QB * JB, NOCC)
    vo = chol_vo.transpose(0, 2, 1).reshape(QB * AB, NOCC)
    am = amplitudes.T.reshape(AB // 8, 8, NOCC)
    dma = pltpu.SemaphoreType.DMA
    return pl.pallas_call(
        kernel,
        out_shape=(jax.ShapeDtypeStruct((QB, JB, NVIRT), BF), jax.ShapeDtypeStruct((JB, NVIRT), F32)),
        in_specs=[pl.BlockSpec(memory_space=pl.ANY)] * 5,
        out_specs=(pl.BlockSpec(memory_space=pl.ANY), pl.BlockSpec(memory_space=pltpu.VMEM)),
        scratch_shapes=[
            pltpu.VMEM((QB * AB, NVIRT), BF),
            pltpu.VMEM((QB * JB, NVIRT), BF),
            pltpu.VMEM((QB * JB, NOCC), BF),
            pltpu.VMEM((QB * AB, NOCC), BF),
            pltpu.VMEM((AB // 8, 8, NOCC), BF),
            pltpu.VMEM((2, NPQ, AB // 8, 8, 128), BF),
            pltpu.VMEM((NVIRT, NOCC), BF),
            pltpu.VMEM((1024, NOCC), F32),
            pltpu.VMEM((NPQ, 8, 1024), BF),
            pltpu.VMEM((2, NPQ, 8, 896), BF),
            pltpu.VMEM((NPQ, 8, 1024), BF),
            pltpu.VMEM((2, NPQ, 8, 896), BF),
            pltpu.VMEM((QB * 8, NOCC), F32),
            pltpu.VMEM((QB * 8, NVIRT), F32),
            pltpu.VMEM((QB, JB, NVIRT), BF),
            pltpu.VMEM((JB, NVIRT), F32),
            pltpu.VMEM((NPB, JB, NVIRT), F32),
            pltpu.VMEM((1, 1, 128), F32),
            pltpu.VMEM((NPQ, 1, 128), F32),
            pltpu.VMEM((QB, 128), F32),
            pltpu.VMEM((QB, 8, 128), F32),
            dma((6,)), dma, dma((NZ - 1,)), dma, dma((NY - 1,)), dma, dma((NY,)),
            dma((3,)), dma((3,)), dma, dma, dma, dma, dma,
        ],
        compiler_params=pltpu.CompilerParams(
            collective_id=0, has_side_effects=True, vmem_limit_bytes=60 * 1024 * 1024),
    )(vv, ov, oo, vo, am)


def solution(mesh):
    in_specs = (
        P("pb", "pq", None),
        P("pb", "pq", None),
        P("pb", "pq", None),
        P("pb", None, "pq"),
        P(None, "pq"),
    )
    out_specs = (P("pb", "pq", None), P("pq", None))
    return jax.shard_map(
        per_device, mesh=mesh, in_specs=in_specs, out_specs=out_specs, check_vma=False
    )
```

time: 157 us -> 76.4 us (0.49)
  Pallas kernels: 0 us -> 72.6 us
  blocking collectives: 67.6 us -> 0 us
  local copies, waits for them, and re-layouts: 39.2 us -> 3.06 us
  waiting for transfers between devices: 19.5 us -> 0 us
  starting transfers between devices: 15.4 us -> 0 us
  matrix products: 9.58 us -> 0 us
  other arithmetic: 3.61 us -> 0 us
    pallas_call x0 -> x1, Pallas kernels: none -> 72.6 us  [per_device(): pl.pallas_call(kernel, out_shape=(jax.ShapeDtypeStruct((QB, JB, NVIRT), B...]
    all_to_all x3 -> x0, blocking collectives: 67.6 us -> none  [copy_for_each(): return lax.all_to_all(copies, axis, split_axis=0, concat_axis=0, tiled=True)]
    all_to_all x2 -> x0, waiting for transfers between devices: 19.5 us -> none  [the longest x1 19.5 us: per_device(): lax.all_to_all(partial_sum.astype(jnp.bfloat16), 'pq', split_axis=1, conc...]
    all_to_all x2 -> x0, starting transfers between devices: 15.4 us -> none  [the longest x1 9.33 us: per_device(): lax.all_to_all(partial_sum.astype(jnp.bfloat16), 'pq', split_axis=1, conc...]
    convert_element_type x4 -> x0, local copies, waits for them, and re-layouts: 14.8 us -> none  [the longest x2 9.91 us: per_device(): moved_sum = lax.all_to_all(partial_sum.astype(jnp.bfloat16), 'pq', split_...]
    unnamed x10 -> x4, local copies, waits for them, and re-layouts: 17.1 us -> 3.06 us
    dot_general x4 -> x0, matrix products: 9.58 us -> none  [the longest x1 6.27 us: per_device(): jnp.einsum('qab,ib->qia', chol_vv, whole_amps, preferred_element_type=jnp...]
    all_to_all x2 -> x0, local copies, waits for them, and re-layouts: 4.13 us -> none  [per_device(): lax.all_to_all(lprime, 'pq', split_axis=2, concat_axis=1, tiled=True)]
  transfers between devices with their start and end apart: 2 -> 0, of which waited for: 1 -> 0; matrix products, arithmetic and copies ran while one was open for 17% -> 0% of each run, Pallas kernels for 0% -> 0%
where the time goes in v1:
time: 76.4 us; the launch traced here: 76.3 us
  Pallas kernels  72.6 us (95%)
  local copies, waits for them, and re-layouts  3.06 us (4%)
    pallas_call x1, Pallas kernels, per_device(): pl.pallas_call(kernel, out_shape=(jax.ShapeDtypeStruct((QB, JB, NVIRT), B...  72.6 us
    unnamed x4, local copies, waits for them, and re-layouts  3.06 us

profile of v1, /device:TPU:1, one launch (start us, length us, event | category | flops | bytes accessed | tf_op | source)
XLA Modules:
  0.0 76.3 jit_solution(6612212774175660573)
XLA Ops:
  0.6 72.6 %shard_map.68 = (bf16[44,8,1792]{2,1,0:T(8,128)(2,1)}, f32[8,1792]{1,0:T(8,128)}) custom-call(bf16[2464,1792]{1,0:T(8,128)(2,1)} %bitcast.9, bf16[352,1792]{1,0:T(8,128)(2,1)} %bitcast.10, bf16[352,256]{1,0:T(8,128)(2,1)} %bitcast.12, bf16[2464,256]{1,0:T(8,128)(2,1)} %bitcast.11, bf16[7,8,256]{2,1,0:T(8,128)(2,1)} %bitcast.13), custom_call_target="tpu_custom_call" | custom-call | tf_op jit(solution)/shard_map/pallas_call | solution.py:306
  73.2 0.0 copy-start
  73.2 2.4 %copy.9 = bf16[44,8,1792]{2,1,0:T(8,128)(2,1)} copy(bf16[44,8,1792]{2,1,0:T(8,128)(2,1)} %get-tuple-element.4) | data formatting | bytes 2523136
  75.6 0.0 copy-done
  75.7 0.6 copy.10
Async XLA Ops:
  73.2 2.4 %copy-start = (f32[8,1792]{1,0:T(8,128)S(1)}, f32[8,1792]{1,0:T(8,128)}, u32[]{:S(2)}) copy-start(f32[8,1792]{1,0:T(8,128)} %get-tuple-element.5) | copy-start | bytes 172036

commit v2 on v1

--- a/solution.py
+++ b/solution.py
@@ -22,8 +22,8 @@
 
 def kernel(vv, ov, oo, vo, am, dressed, fock_out,
            vv_v, ov_v, oo_v, vo_v, t_own, slots, tmat, dbuf, send_a, send_b, recv_a, recv_b,
-           lp, occ, dr, fock, fock_r, coul_s, coul_r, coul_b, pq,
-           lsem, zsend, zrecv, ysend, yrecv, csend, crecv, msend, mrecv, qsend, qrecv, fsend, frecv, osem):
+           lp, occ, coul_s, coul_r, coul_b, pq, f_t, f_s, f_rs, f_row, f_got, f_all, m_s, m_r,
+           lsem, zsend, zrecv, ysend, yrecv, csend, crecv, msend, mrecv, qsend, qrecv, fsend, frecv):
     pb, me = lax.axis_index("pb"), lax.axis_index("pq")
     z, y = me // NY, me % NY
     half = pb % 2
@@ -112,58 +112,71 @@
     def all_peer(k):
         return lax.rem(z + k // NY, NZ) * NY + lax.rem(y + k % NY, NY)
 
-    def send_chunk(src, dst, c):
+    def send_piece(src, dst, lo, hi, n):
+        lanes = pl.ds(lo, hi - lo)
+
         def body(k, carry):
             peer = all_peer(k)
             pltpu.make_async_remote_copy(
-                src_ref=src.at[peer], dst_ref=dst.at[me], send_sem=msend.at[c], recv_sem=mrecv.at[c],
+                src_ref=src.at[peer, :, lanes], dst_ref=dst.at[me, :, lanes],
+                send_sem=msend.at[n], recv_sem=mrecv.at[n],
                 device_id=(pb, peer), device_id_type=MESH).start()
             return carry
+
         lax.fori_loop(1, NPQ, body, 0)
-        dst[me] = src[me]
+        dst[me, :, lo:hi] = src[me, :, lo:hi]
+
+    def wait_piece(dst, lo, hi, n, sem):
+        part = dst.at[pl.ds(0, NPQ - 1), :, pl.ds(lo, hi - lo)]
+        pltpu.make_async_copy(part, part, sem.at[n]).wait()
 
     for c in loads[1:]:
         c.wait()
     tw = t_own[...].astype(F32).reshape(1, AB // 8, 8, NOCC)
 
-    def direct(row0, steps, q0):
-        def body(s, carry):
-            base = pl.multiple_of(s * ROWS, ROWS)
-            rows = pl.ds(pl.multiple_of(row0 + base, 32), ROWS)
-            d = vo_v[rows, :].astype(F32) + jnp.dot(vv_v[rows, :], tmat[...], preferred_element_type=F32)
-            dbuf[pl.ds(base, ROWS), :] = d
-            w = jnp.sum(d.reshape(ROWS // AB, AB // 8, 8, NOCC) * tw, axis=1)
-            pq[pl.ds(q0 + s * (ROWS // AB), ROWS // AB)] = w[:, :, :128] + w[:, :, 128:]
-            return carry
-        lax.fori_loop(0, steps, body, 0)
-
-    def ship(tiles, store):
+    def direct(row0, at, q0):
+        rows = pl.ds(pl.multiple_of(row0, 32), ROWS)
+        d = vo_v[rows, :].astype(F32) + jnp.dot(vv_v[rows, :], tmat[...], preferred_element_type=F32)
+        dbuf[pl.ds(pl.multiple_of(at, 32), ROWS), :] = d
+        vo_v[rows, :] = d.astype(BF)
+        w = jnp.sum(d.reshape(ROWS // AB, AB // 8, 8, NOCC) * tw, axis=1)
+        pq[pl.ds(q0, ROWS // AB)] = w[:, :, :128] + w[:, :, 128:]
+
+    def ship(lo, hi, store):
         def body(t, carry):
             at = pl.multiple_of(t * 128, 128)
             store(at, dbuf[pl.ds(at, 128), :].T.reshape(NPQ, 8, 128).astype(BF))
             return carry
-        lax.fori_loop(0, tiles, body, 0)
+        lax.fori_loop(lo, hi, body, 0)
+
+    def store_a(at, v):
+        send_a[:, :, pl.ds(at, 128)] = v
 
     lpr = oo_v[...].astype(F32) + jnp.dot(ov_v[...], tmat[...], preferred_element_type=F32)
     dbuf[LP_OFF:LP_OFF + 352, :] = lpr
-    direct(0, 3, 0)
-
-    def store_a(at, v):
-        send_a[:, :, pl.ds(at, 128)] = v
-
-    ship(8, store_a)
-    send_chunk(send_a, recv_a, 0)
+    direct(448, 448, 8)
+    ship(4, 8, store_a)
+    send_piece(send_a, recv_a, 512, 1024, 0)
     lpr = dbuf[LP_OFF:LP_OFF + 352, :].astype(BF).astype(F32)
+    direct(0, 0, 0)
+    direct(224, 224, 4)
+    ship(0, 4, store_a)
+    send_piece(send_a, recv_a, 0, 512, 1)
 
     def rest(c, carry):
-        direct(672 + 896 * c, 4, 12 + 16 * c)
+        def step(s, carry2):
+            direct(672 + 896 * c + s * ROWS, s * ROWS, 12 + 16 * c + 4 * s)
+            return carry2
+
+        lax.fori_loop(0, 4, step, 0)
 
         def store_b(at, v):
             send_b[c, :, :, pl.ds(at, 128)] = v
 
-        ship(7, store_b)
-        send_chunk(send_b.at[c], recv_b.at[c], 1 + c)
+        ship(0, 7, store_b)
         return carry
+
+    lax.fori_loop(0, 2, rest, 0)
 
     pick = (lax.broadcasted_iota(jnp.int32, (8, NOCC), 1)
             == me * 8 + lax.broadcasted_iota(jnp.int32, (8, NOCC), 0)).astype(BF)
@@ -171,31 +184,60 @@
     gram = jnp.dot(own_rows, tmat[...], preferred_element_type=F32)
     w = lpr.reshape(QB, 8, NOCC) * gram[None]
     w = w[:, :, :128] + w[:, :, 128:]
-    lax.fori_loop(0, 2, rest, 0)
-
     tot = jnp.sum(pq[...] - w, axis=1)
     tot = jnp.sum(tot, axis=1, keepdims=True)
     eye_q = (lax.broadcasted_iota(jnp.int32, (QB, 128), 0)
              == lax.broadcasted_iota(jnp.int32, (QB, 128), 1)).astype(F32)
     coul_s[0] = jnp.sum(eye_q * tot, axis=0, keepdims=True)
 
-    def q_send(k, carry):
-        peer = all_peer(k)
-        pltpu.make_async_remote_copy(
-            src_ref=coul_s.at[0], dst_ref=coul_r.at[me], send_sem=qsend, recv_sem=qrecv,
-            device_id=(pb, peer), device_id_type=MESH).start()
-        return carry
-
-    lax.fori_loop(1, NPQ, q_send, 0)
+    def row_sends(src, dst, ssem, rsem):
+        def body(k, carry):
+            peer = all_peer(k)
+            pltpu.make_async_remote_copy(
+                src_ref=src(peer), dst_ref=dst.at[me], send_sem=ssem, recv_sem=rsem,
+                device_id=(pb, peer), device_id_type=MESH).start()
+            return carry
+        lax.fori_loop(1, NPQ, body, 0)
+
+    row_sends(lambda peer: coul_s.at[0], coul_r, qsend, qrecv)
     coul_r[me] = coul_s[0]
+    send_piece(send_b.at[0], recv_b.at[0], 0, 896, 2)
+
+    rows_31 = coul_r.at[pl.ds(0, NPQ - 1)]
+    pltpu.make_async_copy(rows_31, rows_31, qrecv).wait()
+    coul = 2.0 * jnp.sum(coul_r[...].reshape(NPQ, 128), axis=0, keepdims=True)
+    coul_b[...] = jnp.broadcast_to(jnp.sum(eye_q * coul, axis=1, keepdims=True), (QB, 128))
+
+    def cq2(q):
+        row = coul_b[pl.ds(q, 1), :]
+        return jnp.concatenate([row, row], axis=1)
+
+    def f_add(u, acc):
+        x = vo_v[pl.ds(pl.multiple_of(u * 2 * AB, 16), 2 * AB), :].astype(F32)
+        return acc + cq2(2 * u) * x[:AB] + cq2(2 * u + 1) * x[AB:]
+
+    acc = lax.fori_loop(0, QB // 2, f_add, jnp.zeros((AB, NOCC), F32))
+    f_t[...] = jnp.concatenate([acc, jnp.zeros((128 - AB, NOCC), F32)], axis=0).T
+    for r in range(8):
+        f_s[r] = f_t[pl.ds(r, NPQ, stride=8), :]
+
+    def pb_sends(src, dst, n):
+        for d in range(1, NPB):
+            to = lax.rem(pb + d, NPB)
+            pltpu.make_async_remote_copy(
+                src_ref=src(to), dst_ref=dst.at[pb], send_sem=fsend.at[n], recv_sem=frecv.at[n],
+                device_id=(to, me), device_id_type=MESH).start()
+
+    def pb_wait(dst, n, sem):
+        part = dst.at[pl.ds(0, NPB - 1)]
+        pltpu.make_async_copy(part, part, sem.at[n]).wait()
+
+    pb_sends(lambda to: f_s.at[to], f_rs, 0)
+    f_rs[pb] = f_s[pb]
 
     lane = lax.broadcasted_iota(jnp.int32, (8, 128), 1)
 
-    def wait_chunk(dst, c):
-        part = dst.at[pl.ds(0, NPQ - 1)]
-        pltpu.make_async_copy(part, part, mrecv.at[c]).wait()
-
-    wait_chunk(recv_a, 0)
+    wait_piece(recv_a, 512, 1024, 0, mrecv)
 
     def lp_row(q, carry):
         start = LP_OFF + 8 * q
@@ -211,19 +253,29 @@
         return carry
 
     lax.fori_loop(0, QB, lp_row, 0)
+
+    def m_add(q, acc):
+        return acc + cq2(q) * lp[pl.ds(pl.multiple_of(q * 8, 8), 8), :]
+
+    m_s[...] = lax.fori_loop(0, QB, m_add, jnp.zeros((8, NOCC), F32))
+    pb_sends(lambda to: m_s, m_r, 1)
+    m_r[pb] = m_s[...]
+
+    pb_wait(f_rs, 0, frecv)
+    tot_f = jnp.sum(f_rs[...], axis=0)
+    f_row[...] = tot_f.reshape(NPQ, 1, 128)
+    row_sends(lambda peer: f_row.at[peer], f_got, fsend.at[2], frecv.at[2])
+    f_got[me] = f_row[me]
+    send_piece(send_b.at[1], recv_b.at[1], 0, 640, 3)
+    send_piece(send_b.at[1], recv_b.at[1], 640, 896, 4)
+
     for n in range(7):
         occ[:, 256 * n:256 * n + 256] = dot_t(lp[...].astype(BF), tmat[256 * n:256 * n + 256, :])
 
-    pltpu.make_async_copy(coul_r.at[pl.ds(0, NPQ - 1)], coul_r.at[pl.ds(0, NPQ - 1)], qrecv).wait()
-    coul = 2.0 * jnp.sum(coul_r[...].reshape(NPQ, 128), axis=0, keepdims=True)
-    coul_b[...] = jnp.broadcast_to(jnp.sum(eye_q * coul, axis=1, keepdims=True), (QB, 128))
-
-    fock[...] = jnp.zeros((8, NVIRT), F32)
-
-    def gather_q(load, ql, q):
+    def gather_q(load, ql, q, last):
         start = AB * ql
         at = pl.multiple_of(start // 128 * 128, 128)
-        nxt = pl.multiple_of(lax.min(at + 128, 768), 128)
+        nxt = pl.multiple_of(lax.min(at + 128, last), 128)
         off = start % 128
         tiles = [None] * 14
         for p in range(NPQ):
@@ -240,60 +292,73 @@
                 tiles[t] = jnp.where(lane >= o, v, tiles[t])
             if o + AB > 128:
                 tiles[t + 1] = v
-        cq = coul_b[pl.ds(q, 1), :]
         rows = pl.ds(pl.multiple_of(q * 8, 8), 8)
         for t in range(14):
             sl = slice(128 * t, 128 * t + 128)
-            d = (tiles[t] - occ[rows, sl]).astype(BF)
-            dr[q, :, sl] = d
-            fock[:, sl] += cq * d.astype(F32)
+            dressed[q, :, sl] = (tiles[t] - occ[rows, sl]).astype(BF)
 
     def do_a(ql, carry):
-        gather_q(lambda p, at: recv_a[p, :, pl.ds(at, 128)].astype(F32), ql, ql)
+        gather_q(lambda p, at: recv_a[p, :, pl.ds(at, 128)].astype(F32), ql, ql, 768)
         return carry
 
+    wait_piece(recv_a, 0, 512, 1, mrecv)
     lax.fori_loop(0, 12, do_a, 0)
 
-    def do_b(c, carry):
-        wait_chunk(recv_b.at[c], 1 + c)
-
-        def inner(ql, carry2):
-            gather_q(lambda p, at: recv_b[c, p, :, pl.ds(at, 128)].astype(F32), ql, 12 + 16 * c + ql)
-            return carry2
-
-        lax.fori_loop(0, 16, inner, 0)
-        return carry
-
-    lax.fori_loop(0, 2, do_b, 0)
-
-    out = pltpu.make_async_copy(dr, dressed, osem)
-    out.start()
-
-    def f_copy(d):
-        return pltpu.make_async_remote_copy(
-            src_ref=fock, dst_ref=fock_r.at[pb], send_sem=fsend, recv_sem=frecv,
-            device_id=(lax.rem(pb + d, NPB), me), device_id_type=MESH)
-
-    for d in range(1, NPB):
-        f_copy(d).start()
-    fock_r[pb] = fock[...]
-    part = fock_r.at[pl.ds(0, NPB - 1)]
-    pltpu.make_async_copy(part, part, frecv).wait()
-    fock_out[...] = jnp.sum(fock_r[...], axis=0) * (1.0 / (QB * NPB))
-
-    out.wait()
+    def do_b(c, last):
+        def inner(ql, carry):
+            gather_q(lambda p, at: recv_b[c, p, :, pl.ds(at, 128)].astype(F32), ql, 12 + 16 * c + ql, last)
+            return carry
+        return inner
+
+    wait_piece(recv_b.at[0], 0, 896, 2, mrecv)
+    lax.fori_loop(0, 16, do_b(0, 768), 0)
+
+    got_31 = f_got.at[pl.ds(0, NPQ - 1)]
+    pltpu.make_async_copy(got_31, got_31, frecv.at[2]).wait()
+    pb_sends(lambda to: f_got, f_all, 3)
+    f_all[pb] = f_got[...]
+    pb_wait(m_r, 1, frecv)
+    m = jnp.sum(m_r[...], axis=0)
+    m_hi = m.astype(BF)
+    m_lo = m - m_hi.astype(F32)
+    m_mid = m_lo.astype(BF)
+    m_low = (m_lo - m_mid.astype(F32)).astype(BF)
+    f_occ = dot_t(m_hi, tmat[...]) + (dot_t(m_mid, tmat[...]) + dot_t(m_low, tmat[...]))
+    pb_wait(f_all, 3, frecv)
+    ftiles = [None] * 14
+    for p in range(NPQ):
+        o, t = AB * p % 128, AB * p // 128
+        v = f_all[:, p].reshape(NPB, 128)
+        if o:
+            v = pltpu.roll(v, o, 1)
+        ftiles[t] = v if ftiles[t] is None else jnp.where(lane >= o, v, ftiles[t])
+        if o + AB > 128:
+            ftiles[t + 1] = v
+    for t in range(14):
+        sl = slice(128 * t, 128 * t + 128)
+        fock_out[:, sl] = (ftiles[t] - f_occ[:, sl]) * (1.0 / (QB * NPB))
+
+    wait_piece(recv_b.at[1], 0, 640, 3, mrecv)
+    lax.fori_loop(0, 11, do_b(1, 512), 0)
+    wait_piece(recv_b.at[1], 640, 896, 4, mrecv)
+    lax.fori_loop(11, 16, do_b(1, 768), 0)
+
     zs = slots.at[0, pl.ds(0, NZ - 1)]
     pltpu.make_async_copy(zs, zs, zsend).wait()
     ys = slots.at[0, pl.ds(0, NZ * (NY - 1))]
     pltpu.make_async_copy(ys, ys, ysend).wait()
     cs = slots.at[0]
     pltpu.make_async_copy(cs, cs, csend).wait()
-    for c, src in ((0, recv_a), (1, recv_b.at[0]), (2, recv_b.at[1])):
-        sp = src.at[pl.ds(0, NPQ - 1)]
-        pltpu.make_async_copy(sp, sp, msend.at[c]).wait()
-    qp = coul_r.at[pl.ds(0, NPQ - 1)]
-    pltpu.make_async_copy(qp, qp, qsend).wait()
-    pltpu.make_async_copy(part, part, fsend).wait()
+    wait_piece(recv_a, 512, 1024, 0, msend)
+    wait_piece(recv_a, 0, 512, 1, msend)
+    wait_piece(recv_b.at[0], 0, 896, 2, msend)
+    wait_piece(recv_b.at[1], 0, 640, 3, msend)
+    wait_piece(recv_b.at[1], 640, 896, 4, msend)
+    pltpu.make_async_copy(rows_31, rows_31, qsend).wait()
+    pltpu.make_async_copy(got_31, got_31, fsend.at[2]).wait()
+    pb_wait(f_rs, 0, fsend)
+    pb_wait(m_r, 1, fsend)
+    pb_wait(f_all, 3, fsend)
 
 
 def per_device(chol_vv, chol_ov, chol_oo, chol_vo, amplitudes):
@@ -303,11 +368,12 @@
     vo = chol_vo.transpose(0, 2, 1).reshape(QB * AB, NOCC)
     am = amplitudes.T.reshape(AB // 8, 8, NOCC)
     dma = pltpu.SemaphoreType.DMA
+    vv, ov, oo, vo, am = (pltpu.with_memory_space_constraint(x, pltpu.HBM) for x in (vv, ov, oo, vo, am))
     return pl.pallas_call(
         kernel,
         out_shape=(jax.ShapeDtypeStruct((QB, JB, NVIRT), BF), jax.ShapeDtypeStruct((JB, NVIRT), F32)),
-        in_specs=[pl.BlockSpec(memory_space=pl.ANY)] * 5,
-        out_specs=(pl.BlockSpec(memory_space=pl.ANY), pl.BlockSpec(memory_space=pltpu.VMEM)),
+        in_specs=[pl.BlockSpec(memory_space=pltpu.HBM)] * 5,
+        out_specs=[pl.BlockSpec(memory_space=pltpu.VMEM)] * 2,
         scratch_shapes=[
             pltpu.VMEM((QB * AB, NVIRT), BF),
             pltpu.VMEM((QB * JB, NVIRT), BF),
@@ -323,18 +389,23 @@
             pltpu.VMEM((2, NPQ, 8, 896), BF),
             pltpu.VMEM((QB * 8, NOCC), F32),
             pltpu.VMEM((QB * 8, NVIRT), F32),
-            pltpu.VMEM((QB, JB, NVIRT), BF),
-            pltpu.VMEM((JB, NVIRT), F32),
-            pltpu.VMEM((NPB, JB, NVIRT), F32),
             pltpu.VMEM((1, 1, 128), F32),
             pltpu.VMEM((NPQ, 1, 128), F32),
             pltpu.VMEM((QB, 128), F32),
             pltpu.VMEM((QB, 8, 128), F32),
+            pltpu.VMEM((NOCC, 128), F32),
+            pltpu.VMEM((NPB, NPQ, 128), F32),
+            pltpu.VMEM((NPB, NPQ, 128), F32),
+            pltpu.VMEM((NPQ, 1, 128), F32),
+            pltpu.VMEM((NPQ, 1, 128), F32),
+            pltpu.VMEM((NPB, NPQ, 1, 128), F32),
+            pltpu.VMEM((JB, NOCC), F32),
+            pltpu.VMEM((NPB, JB, NOCC), F32),
             dma((6,)), dma, dma((NZ - 1,)), dma, dma((NY - 1,)), dma, dma((NY,)),
-            dma((3,)), dma((3,)), dma, dma, dma, dma, dma,
+            dma((5,)), dma((5,)), dma, dma, dma((4,)), dma((4,)),
         ],
         compiler_params=pltpu.CompilerParams(
-            collective_id=0, has_side_effects=True, vmem_limit_bytes=60 * 1024 * 1024),
+            collective_id=0, has_side_effects=True, vmem_limit_bytes=34 * 1024 * 1024),
     )(vv, ov, oo, vo, am)
 
 

time: 76.4 us -> 63.3 us (0.83)
  Pallas kernels: 72.6 us -> 61 us
  local copies, waits for them, and re-layouts: 3.06 us -> 1.66 us
    pallas_call x1, Pallas kernels: 72.6 us -> 61 us  [per_device(): pl.pallas_call(kernel, out_shape=(jax.ShapeDtypeStruct((QB, JB, NVIRT), B...]
    unnamed x4 -> x2, local copies, waits for them, and re-layouts: 3.06 us -> 1.66 us
where the time goes in v2:
time: 63.3 us
  Pallas kernels  61 us (96%)
  local copies, waits for them, and re-layouts  1.66 us (3%)
  between operations  0.64 us (1%)
    pallas_call x1, Pallas kernels, per_device(): pl.pallas_call(kernel, out_shape=(jax.ShapeDtypeStruct((QB, JB, NVIRT), B...  61 us
    unnamed x2, local copies, waits for them, and re-layouts  1.66 us

profile of v2, /device:TPU:1, one launch (start us, length us, event | category | flops | bytes accessed | tf_op | source)
XLA Modules:
  0.0 63.3 jit_solution(8551714518416930277)
XLA Ops:
  0.6 61.0 %shard_map.68 = (bf16[44,8,1792]{2,1,0:T(8,128)(2,1)S(1)}, f32[8,1792]{1,0:T(8,128)S(1)}) custom-call(bf16[2464,1792]{1,0:T(8,128)(2,1)} %bitcast.9, bf16[352,1792]{1,0:T(8,128)(2,1)} %bitcast.10, bf16[352,256]{1,0:T(8,128)(2,1)} %bitcast.12, bf16[2464,256]{1,0:T(8,128)(2,1)} %bitcast.11, bf16[7,8,256]{2,1,0:T(8,128)(2,1)} %bitcast.13), custom_call_target="tpu_custom_call" | custom-call | tf_op jit(solution)/shard_map/pallas_call | solution.py:372
  61.6 1.0 %copy.9 = bf16[44,8,1792]{2,1,0:T(8,128)(2,1)} copy(bf16[44,8,1792]{2,1,0:T(8,128)(2,1)S(1)} %get-tuple-element.4) | data formatting | bytes 2523136
  62.6 0.6 copy.10

commit v3 on v2

--- a/solution.py
+++ b/solution.py
@@ -12,8 +12,24 @@
 NOCC, NVIRT, QB = 256, 1792, 44
 AB, JB = NVIRT // NPQ, NOCC // NPQ
 LP_OFF = 672
-ROWS = 224
 ZORDER = (1, 7, 2, 6, 3, 5, 4)
+
+
+def position(d):
+    z, y = d // NY, d % NY
+    return (y % 2) * 16 + z * 2 + y // 2
+
+
+def owner(k):
+    return (k % 16) // 2 * NY + k % 2 * 2 + k // 16
+
+
+def place_matrix():
+    a = lax.broadcasted_iota(jnp.int32, (NOCC, NOCC), 0)
+    b = lax.broadcasted_iota(jnp.int32, (NOCC, NOCC), 1)
+    d = a // 8
+    to = (d % 2) * 16 + d // NY * 2 + d % NY // 2
+    return (b == to * 8 + a % 8).astype(BF)
 
 
 def dot_t(a, b):
@@ -21,7 +37,7 @@
 
 
 def kernel(vv, ov, oo, vo, am, dressed, fock_out,
-           vv_v, ov_v, oo_v, vo_v, t_own, slots, tmat, dbuf, send_a, send_b, recv_a, recv_b,
+           vv_v, ov_v, oo_v, vo_v, am_v, t_own, slots, tmat, lp_own, send_a, send_b, recv_a, recv_b,
            lp, occ, coul_s, coul_r, coul_b, pq, f_t, f_s, f_rs, f_row, f_got, f_all, m_s, m_r,
            lsem, zsend, zrecv, ysend, yrecv, csend, crecv, msend, mrecv, qsend, qrecv, fsend, frecv):
     pb, me = lax.axis_index("pb"), lax.axis_index("pq")
@@ -45,17 +61,33 @@
 
     own_slot = y * NZ + z
     loads = [
-        pltpu.make_async_copy(
-            am.at[:, :, pl.ds(pl.multiple_of(128 * half, 128), 128)], slots.at[half, own_slot], lsem.at[0]),
-        pltpu.make_async_copy(am, t_own, lsem.at[1]),
-        pltpu.make_async_copy(oo, oo_v, lsem.at[2]),
-        pltpu.make_async_copy(ov, ov_v, lsem.at[3]),
-        pltpu.make_async_copy(vo, vo_v, lsem.at[4]),
-        pltpu.make_async_copy(vv, vv_v, lsem.at[5]),
+        pltpu.make_async_copy(am, am_v, lsem.at[0]),
+        pltpu.make_async_copy(oo, oo_v, lsem.at[1]),
+        pltpu.make_async_copy(ov, ov_v, lsem.at[2]),
+        pltpu.make_async_copy(vo, vo_v, lsem.at[3]),
+        pltpu.make_async_copy(vv, vv_v, lsem.at[4]),
     ]
     for c in loads:
         c.start()
     loads[0].wait()
+    shuffle = place_matrix()
+    own = jnp.dot(am_v[...], shuffle, preferred_element_type=F32)
+    for k in range(AB // 8):
+        t_own[k] = own[8 * k:8 * k + 8].astype(BF)
+        for hh in range(2):
+            @pl.when(half == hh)
+            def _():
+                slots[hh, own_slot, k] = own[8 * k:8 * k + 8, 128 * hh:128 * hh + 128].astype(BF)
+    loads[1].wait()
+    oo_v[...] = jnp.dot(oo_v[...], shuffle, preferred_element_type=F32).astype(BF)
+    loads[3].wait()
+
+    def shuffle_vo(c, carry):
+        rows = pl.ds(pl.multiple_of(c * 352, 32), 352)
+        vo_v[rows, :] = jnp.dot(vo_v[rows, :], shuffle, preferred_element_type=F32).astype(BF)
+        return carry
+
+    lax.fori_loop(0, 7, shuffle_vo, 0)
     pl.semaphore_wait(bar, (NZ - 1) + (NY - 1) + (NPB - 1))
 
     def z_copy(d):
@@ -91,23 +123,23 @@
         group = pl.ds(lax.rem(y + NY - e, NY) * NZ, NZ)
         pltpu.make_async_copy(slots.at[half, group], slots.at[half, group], yrecv.at[e - 1]).wait()
         c_copy(e).start()
-    for e in range(NY):
-        group = pl.ds(lax.rem(y + NY - e, NY) * NZ, NZ)
-        pltpu.make_async_copy(slots.at[1 - half, group], slots.at[1 - half, group], crecv.at[e]).wait()
-
-    def widen(u, carry):
-        for hh in range(2):
+    def widen(hh):
+        cols = pl.ds(pl.multiple_of(128 * hh, 128), 128)
+
+        def body(u, carry):
             for k in range(7):
                 parts = []
                 for g in (2 * k, 2 * k + 1):
                     p = 2 * u + g // 7
                     slot = lax.rem(p, NY) * NZ + p // NY
                     parts.append(slots[hh, slot, g % 7].astype(F32))
-                tmat[pl.ds(pl.multiple_of(112 * u + 16 * k, 16), 16), 128 * hh:128 * hh + 128] = (
+                tmat[pl.ds(pl.multiple_of(112 * u + 16 * k, 16), 16), cols] = (
                     jnp.concatenate(parts, axis=0).astype(BF))
-        return carry
-
-    lax.fori_loop(0, NPQ // 2, widen, 0)
+            return carry
+
+        lax.fori_loop(0, NPQ // 2, body, 0)
+
+    widen(half)
 
     def all_peer(k):
         return lax.rem(z + k // NY, NZ) * NY + lax.rem(y + k % NY, NY)
@@ -118,68 +150,85 @@
         def body(k, carry):
             peer = all_peer(k)
             pltpu.make_async_remote_copy(
-                src_ref=src.at[peer, :, lanes], dst_ref=dst.at[me, :, lanes],
+                src_ref=src.at[position(peer), :, lanes], dst_ref=dst.at[me, :, lanes],
                 send_sem=msend.at[n], recv_sem=mrecv.at[n],
                 device_id=(pb, peer), device_id_type=MESH).start()
             return carry
 
         lax.fori_loop(1, NPQ, body, 0)
-        dst[me, :, lo:hi] = src[me, :, lo:hi]
+        dst[me, :, lo:hi] = src[position(me), :, lo:hi]
+
+    def send_half(src, dst, lo, hi, n, hh):
+        lanes = pl.ds(lo, hi - lo)
+
+        def body(k, carry):
+            peer = all_peer(2 * k + lax.rem(y + hh, 2))
+
+            @pl.when(peer != me)
+            def _():
+                pltpu.make_async_remote_copy(
+                    src_ref=src.at[position(peer), :, lanes], dst_ref=dst.at[me, :, lanes],
+                    send_sem=msend.at[n], recv_sem=mrecv.at[n],
+                    device_id=(pb, peer), device_id_type=MESH).start()
+            return carry
+
+        lax.fori_loop(0, 16, body, 0)
 
     def wait_piece(dst, lo, hi, n, sem):
         part = dst.at[pl.ds(0, NPQ - 1), :, pl.ds(lo, hi - lo)]
         pltpu.make_async_copy(part, part, sem.at[n]).wait()
 
-    for c in loads[1:]:
-        c.wait()
-    tw = t_own[...].astype(F32).reshape(1, AB // 8, 8, NOCC)
-
-    def direct(row0, at, q0):
-        rows = pl.ds(pl.multiple_of(row0, 32), ROWS)
-        d = vo_v[rows, :].astype(F32) + jnp.dot(vv_v[rows, :], tmat[...], preferred_element_type=F32)
-        dbuf[pl.ds(pl.multiple_of(at, 32), ROWS), :] = d
-        vo_v[rows, :] = d.astype(BF)
-        w = jnp.sum(d.reshape(ROWS // AB, AB // 8, 8, NOCC) * tw, axis=1)
-        pq[pl.ds(q0, ROWS // AB)] = w[:, :, :128] + w[:, :, 128:]
-
-    def ship(lo, hi, store):
-        def body(t, carry):
-            at = pl.multiple_of(t * 128, 128)
-            store(at, dbuf[pl.ds(at, 128), :].T.reshape(NPQ, 8, 128).astype(BF))
-            return carry
-        lax.fori_loop(lo, hi, body, 0)
-
-    def store_a(at, v):
-        send_a[:, :, pl.ds(at, 128)] = v
-
-    lpr = oo_v[...].astype(F32) + jnp.dot(ov_v[...], tmat[...], preferred_element_type=F32)
-    dbuf[LP_OFF:LP_OFF + 352, :] = lpr
-    direct(448, 448, 8)
-    ship(4, 8, store_a)
-    send_piece(send_a, recv_a, 512, 1024, 0)
-    lpr = dbuf[LP_OFF:LP_OFF + 352, :].astype(BF).astype(F32)
-    direct(0, 0, 0)
-    direct(224, 224, 4)
-    ship(0, 4, store_a)
-    send_piece(send_a, recv_a, 0, 512, 1)
+    loads[2].wait()
+    loads[4].wait()
+    def direct(row0, n, q0, cols, old=None):
+        rows = pl.ds(pl.multiple_of(row0, 32), n)
+        d = vo_v[rows, cols].astype(F32) + jnp.dot(vv_v[rows, :], tmat[:, cols], preferred_element_type=F32)
+        vo_v[rows, cols] = d.astype(BF)
+        w = jnp.sum(d.reshape(n // AB, AB // 8, 8, d.shape[1]) * t_own[:, :, cols].astype(F32)[None], axis=1)
+        if d.shape[1] == NOCC:
+            w = w[:, :, :128] + w[:, :, 128:]
+        here = pl.ds(q0, n // AB)
+        pq[here] = w if old is None else pq[here] + w
+
+    def first_chunk(hh, old):
+        cols = pl.ds(pl.multiple_of(128 * hh, 128), 128)
+        owners = pl.ds(16 * hh, 16)
+
+        def ship(at, block):
+            send_a[owners, :, pl.ds(at, 128)] = block.astype(F32).T.reshape(16, 8, 128).astype(BF)
+
+        lp_own[:, cols] = (oo_v[:, cols].astype(F32) + jnp.dot(
+            ov_v[...], tmat[:, cols], preferred_element_type=F32)).astype(BF)
+        direct(448, 224, 8, cols, old)
+        ship(512, vo_v[512:640, cols])
+        ship(640, jnp.concatenate([vo_v[640:672, cols], lp_own[0:96, cols]], axis=0))
+        ship(768, lp_own[96:224, cols])
+        ship(896, lp_own[224:352, cols])
+        if old is None:
+            send_half(send_a, recv_a, 512, 1024, 0, hh)
+        direct(0, 448, 0, cols, old)
+        for t in range(4):
+            ship(128 * t, vo_v[128 * t:128 * t + 128, cols])
+        if old is None:
+            send_half(send_a, recv_a, 0, 512, 1, hh)
+
+    first_chunk(half, None)
+    for e in range(NY):
+        group = pl.ds(lax.rem(y + NY - e, NY) * NZ, NZ)
+        pltpu.make_async_copy(slots.at[1 - half, group], slots.at[1 - half, group], crecv.at[e]).wait()
+    widen(1 - half)
+    first_chunk(1 - half, True)
+    recv_a[me] = send_a[position(me)]
+    lpr = lp_own[...].astype(F32)
 
     def rest(c, carry):
-        def step(s, carry2):
-            direct(672 + 896 * c + s * ROWS, s * ROWS, 12 + 16 * c + 4 * s)
-            return carry2
-
-        lax.fori_loop(0, 4, step, 0)
-
-        def store_b(at, v):
-            send_b[c, :, :, pl.ds(at, 128)] = v
-
-        ship(0, 7, store_b)
+        direct(672 + 448 * c, 448, 12 + 8 * c, slice(0, NOCC))
         return carry
 
-    lax.fori_loop(0, 2, rest, 0)
+    lax.fori_loop(0, 4, rest, 0)
 
     pick = (lax.broadcasted_iota(jnp.int32, (8, NOCC), 1)
-            == me * 8 + lax.broadcasted_iota(jnp.int32, (8, NOCC), 0)).astype(BF)
+            == position(me) * 8 + lax.broadcasted_iota(jnp.int32, (8, NOCC), 0)).astype(BF)
     own_rows = dot_t(pick, tmat[...]).astype(BF)
     gram = jnp.dot(own_rows, tmat[...], preferred_element_type=F32)
     w = lpr.reshape(QB, 8, NOCC) * gram[None]
@@ -201,10 +250,23 @@
 
     row_sends(lambda peer: coul_s.at[0], coul_r, qsend, qrecv)
     coul_r[me] = coul_s[0]
-    send_piece(send_b.at[0], recv_b.at[0], 0, 896, 2)
+    send_half(send_a, recv_a, 512, 1024, 0, 1 - half)
+    send_half(send_a, recv_a, 0, 512, 1, 1 - half)
+
+    def ship_b(c):
+        def body(t, carry):
+            at = pl.multiple_of(t * 128, 128)
+            block = vo_v[pl.ds(pl.multiple_of(672 + 896 * c + at, 32), 128), :].astype(F32)
+            send_b[c, :, :, pl.ds(at, 128)] = block.T.reshape(NPQ, 8, 128).astype(BF)
+            return carry
+        lax.fori_loop(0, 7, body, 0)
+
+    ship_b(0)
+    ship_b(1)
 
     rows_31 = coul_r.at[pl.ds(0, NPQ - 1)]
     pltpu.make_async_copy(rows_31, rows_31, qrecv).wait()
+    send_piece(send_b.at[0], recv_b.at[0], 0, 896, 2)
     coul = 2.0 * jnp.sum(coul_r[...].reshape(NPQ, 128), axis=0, keepdims=True)
     coul_b[...] = jnp.broadcast_to(jnp.sum(eye_q * coul, axis=1, keepdims=True), (QB, 128))
 
@@ -246,7 +308,7 @@
         for hh in range(2):
             acc = None
             for g in range(16):
-                v = recv_a[16 * hh + g, :, pl.ds(at, 128)].astype(F32)
+                v = recv_a[owner(16 * hh + g), :, pl.ds(at, 128)].astype(F32)
                 v = pltpu.roll(v, lax.rem(8 * g - off + 128, 128), 1)
                 acc = v if acc is None else jnp.where(lane >= 8 * g, v, acc)
             lp[pl.ds(pl.multiple_of(q * 8, 8), 8), 128 * hh:128 * hh + 128] = acc
@@ -264,8 +326,8 @@
     pb_wait(f_rs, 0, frecv)
     tot_f = jnp.sum(f_rs[...], axis=0)
     f_row[...] = tot_f.reshape(NPQ, 1, 128)
-    row_sends(lambda peer: f_row.at[peer], f_got, fsend.at[2], frecv.at[2])
-    f_got[me] = f_row[me]
+    row_sends(lambda peer: f_row.at[position(peer)], f_got, fsend.at[2], frecv.at[2])
+    f_got[me] = f_row[position(me)]
     send_piece(send_b.at[1], recv_b.at[1], 0, 640, 3)
     send_piece(send_b.at[1], recv_b.at[1], 640, 896, 4)
 
@@ -311,12 +373,15 @@
         return inner
 
     wait_piece(recv_b.at[0], 0, 896, 2, mrecv)
-    lax.fori_loop(0, 16, do_b(0, 768), 0)
-
     got_31 = f_got.at[pl.ds(0, NPQ - 1)]
     pltpu.make_async_copy(got_31, got_31, frecv.at[2]).wait()
     pb_sends(lambda to: f_got, f_all, 3)
     f_all[pb] = f_got[...]
+    lax.fori_loop(0, 16, do_b(0, 768), 0)
+
+    wait_piece(recv_b.at[1], 0, 640, 3, mrecv)
+    lax.fori_loop(0, 11, do_b(1, 512), 0)
+
     pb_wait(m_r, 1, frecv)
     m = jnp.sum(m_r[...], axis=0)
     m_hi = m.astype(BF)
@@ -338,8 +403,6 @@
         sl = slice(128 * t, 128 * t + 128)
         fock_out[:, sl] = (ftiles[t] - f_occ[:, sl]) * (1.0 / (QB * NPB))
 
-    wait_piece(recv_b.at[1], 0, 640, 3, mrecv)
-    lax.fori_loop(0, 11, do_b(1, 512), 0)
     wait_piece(recv_b.at[1], 640, 896, 4, mrecv)
     lax.fori_loop(11, 16, do_b(1, 768), 0)
 
@@ -366,7 +429,7 @@
     ov = chol_ov.reshape(QB * JB, NVIRT)
     oo = chol_oo.reshape(QB * JB, NOCC)
     vo = chol_vo.transpose(0, 2, 1).reshape(QB * AB, NOCC)
-    am = amplitudes.T.reshape(AB // 8, 8, NOCC)
+    am = amplitudes.T
     dma = pltpu.SemaphoreType.DMA
     vv, ov, oo, vo, am = (pltpu.with_memory_space_constraint(x, pltpu.HBM) for x in (vv, ov, oo, vo, am))
     return pl.pallas_call(
@@ -379,10 +442,11 @@
             pltpu.VMEM((QB * JB, NVIRT), BF),
             pltpu.VMEM((QB * JB, NOCC), BF),
             pltpu.VMEM((QB * AB, NOCC), BF),
+            pltpu.VMEM((AB, NOCC), BF),
             pltpu.VMEM((AB // 8, 8, NOCC), BF),
             pltpu.VMEM((2, NPQ, AB // 8, 8, 128), BF),
             pltpu.VMEM((NVIRT, NOCC), BF),
-            pltpu.VMEM((1024, NOCC), F32),
+            pltpu.VMEM((QB * JB, NOCC), BF),
             pltpu.VMEM((NPQ, 8, 1024), BF),
             pltpu.VMEM((2, NPQ, 8, 896), BF),
             pltpu.VMEM((NPQ, 8, 1024), BF),
@@ -401,7 +465,7 @@
             pltpu.VMEM((NPB, NPQ, 1, 128), F32),
             pltpu.VMEM((JB, NOCC), F32),
             pltpu.VMEM((NPB, JB, NOCC), F32),
-            dma((6,)), dma, dma((NZ - 1,)), dma, dma((NY - 1,)), dma, dma((NY,)),
+            dma((5,)), dma, dma((NZ - 1,)), dma, dma((NY - 1,)), dma, dma((NY,)),
             dma((5,)), dma((5,)), dma, dma, dma((4,)), dma((4,)),
         ],
         compiler_params=pltpu.CompilerParams(

time: 63.3 us -> 59.8 us (0.945)
  Pallas kernels: 61 us -> 57.5 us
    pallas_call x1, Pallas kernels: 61 us -> 57.5 us  [per_device(): pl.pallas_call(kernel, out_shape=(jax.ShapeDtypeStruct((QB, JB, NVIRT), B...]
where the time goes in v3:
time: 59.8 us
  Pallas kernels  57.5 us (96%)
  local copies, waits for them, and re-layouts  1.66 us (3%)
  between operations  0.64 us (1%)
    pallas_call x1, Pallas kernels, per_device(): pl.pallas_call(kernel, out_shape=(jax.ShapeDtypeStruct((QB, JB, NVIRT), B...  57.5 us
    unnamed x2, local copies, waits for them, and re-layouts  1.66 us

profile of v3, /device:TPU:1, one launch (start us, length us, event | category | flops | bytes accessed | tf_op | source)
XLA Modules:
  0.0 59.8 jit_solution(11399401458892932005)
XLA Ops:
  0.6 57.5 %shard_map.68 = (bf16[44,8,1792]{2,1,0:T(8,128)(2,1)S(1)}, f32[8,1792]{1,0:T(8,128)S(1)}) custom-call(bf16[2464,1792]{1,0:T(8,128)(2,1)} %bitcast.7, bf16[352,1792]{1,0:T(8,128)(2,1)} %bitcast.8, bf16[352,256]{1,0:T(8,128)(2,1)} %bitcast.10, bf16[2464,256]{1,0:T(8,128)(2,1)} %bitcast.9, bf16[56,256]{1,0:T(8,128)(2,1)} %bitcast.11), custom_call_target="tpu_custom_call" | custom-call | tf_op jit(solution)/shard_map/pallas_call | solution.py:435
  58.1 1.0 %copy.9 = bf16[44,8,1792]{2,1,0:T(8,128)(2,1)} copy(bf16[44,8,1792]{2,1,0:T(8,128)(2,1)S(1)} %get-tuple-element.4) | data formatting | bytes 2523136
  59.1 0.6 %copy.10 = f32[8,1792]{1,0:T(8,128)} copy(f32[8,1792]{1,0:T(8,128)S(1)} %get-tuple-element.5) | data formatting | bytes 114688

commit v4 on v3

--- a/solution.py
+++ b/solution.py
@@ -190,35 +190,36 @@
         here = pl.ds(q0, n // AB)
         pq[here] = w if old is None else pq[here] + w
 
-    def first_chunk(hh, old):
+    def first_chunk(hh, old, compute, move):
         cols = pl.ds(pl.multiple_of(128 * hh, 128), 128)
         owners = pl.ds(16 * hh, 16)
 
         def ship(at, block):
             send_a[owners, :, pl.ds(at, 128)] = block.astype(F32).T.reshape(16, 8, 128).astype(BF)
 
-        lp_own[:, cols] = (oo_v[:, cols].astype(F32) + jnp.dot(
-            ov_v[...], tmat[:, cols], preferred_element_type=F32)).astype(BF)
-        direct(448, 224, 8, cols, old)
-        ship(512, vo_v[512:640, cols])
-        ship(640, jnp.concatenate([vo_v[640:672, cols], lp_own[0:96, cols]], axis=0))
-        ship(768, lp_own[96:224, cols])
-        ship(896, lp_own[224:352, cols])
-        if old is None:
+        if compute:
+            lp_own[:, cols] = (oo_v[:, cols].astype(F32) + jnp.dot(
+                ov_v[...], tmat[:, cols], preferred_element_type=F32)).astype(BF)
+            direct(448, 224, 8, cols, old)
+        if move:
+            ship(512, vo_v[512:640, cols])
+            ship(640, jnp.concatenate([vo_v[640:672, cols], lp_own[0:96, cols]], axis=0))
+            ship(768, lp_own[96:224, cols])
+            ship(896, lp_own[224:352, cols])
             send_half(send_a, recv_a, 512, 1024, 0, hh)
-        direct(0, 448, 0, cols, old)
-        for t in range(4):
-            ship(128 * t, vo_v[128 * t:128 * t + 128, cols])
-        if old is None:
+        if compute:
+            direct(0, 448, 0, cols, old)
+        if move:
+            for t in range(4):
+                ship(128 * t, vo_v[128 * t:128 * t + 128, cols])
             send_half(send_a, recv_a, 0, 512, 1, hh)
 
-    first_chunk(half, None)
+    first_chunk(half, None, True, True)
     for e in range(NY):
         group = pl.ds(lax.rem(y + NY - e, NY) * NZ, NZ)
         pltpu.make_async_copy(slots.at[1 - half, group], slots.at[1 - half, group], crecv.at[e]).wait()
     widen(1 - half)
-    first_chunk(1 - half, True)
-    recv_a[me] = send_a[position(me)]
+    first_chunk(1 - half, True, True, False)
     lpr = lp_own[...].astype(F32)
 
     def rest(c, carry):
@@ -250,8 +251,8 @@
 
     row_sends(lambda peer: coul_s.at[0], coul_r, qsend, qrecv)
     coul_r[me] = coul_s[0]
-    send_half(send_a, recv_a, 512, 1024, 0, 1 - half)
-    send_half(send_a, recv_a, 0, 512, 1, 1 - half)
+    first_chunk(1 - half, True, False, True)
+    recv_a[me] = send_a[position(me)]
 
     def ship_b(c):
         def body(t, carry):

time: 59.8 us -> 59.2 us (0.990)
  Pallas kernels: 57.5 us -> 56.8 us
    pallas_call x1, Pallas kernels: 57.5 us -> 56.8 us  [per_device(): pl.pallas_call(kernel, out_shape=(jax.ShapeDtypeStruct((QB, JB, NVIRT), B...]
where the time goes in v4:
time: 59.2 us; the launch traced here: 59.1 us
  Pallas kernels  56.8 us (96%)
  local copies, waits for them, and re-layouts  1.66 us (3%)
  between operations  0.64 us (1%)
    pallas_call x1, Pallas kernels, per_device(): pl.pallas_call(kernel, out_shape=(jax.ShapeDtypeStruct((QB, JB, NVIRT), B...  56.8 us
    unnamed x2, local copies, waits for them, and re-layouts  1.66 us

profile of v4, /device:TPU:1, one launch (start us, length us, event | category | flops | bytes accessed | tf_op | source)
XLA Modules:
  0.0 59.1 jit_solution(10098142093118065162)
XLA Ops:
  0.6 56.8 %shard_map.68 = (bf16[44,8,1792]{2,1,0:T(8,128)(2,1)S(1)}, f32[8,1792]{1,0:T(8,128)S(1)}) custom-call(bf16[2464,1792]{1,0:T(8,128)(2,1)} %bitcast.7, bf16[352,1792]{1,0:T(8,128)(2,1)} %bitcast.8, bf16[352,256]{1,0:T(8,128)(2,1)} %bitcast.10, bf16[2464,256]{1,0:T(8,128)(2,1)} %bitcast.9, bf16[56,256]{1,0:T(8,128)(2,1)} %bitcast.11), custom_call_target="tpu_custom_call" | custom-call | tf_op jit(solution)/shard_map/pallas_call | solution.py:436
  57.4 1.0 %copy.9 = bf16[44,8,1792]{2,1,0:T(8,128)(2,1)} copy(bf16[44,8,1792]{2,1,0:T(8,128)(2,1)S(1)} %get-tuple-element.4) | data formatting | bytes 2523136
  58.5 0.6 %copy.10 = f32[8,1792]{1,0:T(8,128)} copy(f32[8,1792]{1,0:T(8,128)S(1)} %get-tuple-element.5) | data formatting | bytes 114688
